TPU v7x, 32 devices: a whole 2x2x4 slice. The times are simulated.
32 devices in a mesh: dp: 8 (over z, x), txt: 4 (over y, core).
Axes of the slice: x: 2, y: 2, z: 4, core: 2. Of those that a mesh axis runs over, the one named last changes fastest.
Arguments:
- resid: bfloat16 [2048, 1024], P('dp', 'txt'), may hold values from -40 to 40
- prenorm_gain: float32 [1024], replicated, may hold values from 0.25 to 1.75
- prenorm_bias: float32 [1024], replicated, may hold values from -3 to 3
- up_weight: bfloat16 [1024, 4096], P('dp', 'txt'), may hold values from -0.1875 to 0.1875
- up_bias: float32 [4096], P('txt'), may hold values from -3 to 3
- down_weight: bfloat16 [4096, 1024], P('txt', 'dp'), may hold values from -0.09375 to 0.09375
- down_bias: float32 [1024], replicated, may hold values from -3 to 3
- post_gain: float32 [1024], P('txt'), may hold values from 0.25 to 1.75
- post_bias: float32 [1024], P('txt'), may hold values from -3 to 3
- projection: bfloat16 [1024, 768], P('txt'), may hold values from -1 to 1
- texts: bfloat16 [5120, 768], P('txt'), may hold values from -48 to 48
- labels: int32 [2048], P('dp'), may hold values from 0 to 5119
- step_size: float32 [1], replicated, may hold values from 0.5 to 2
Outputs:
- adversarial: float32 [2048, 1024], P('dp', 'txt')
All inputs are finite; a program needn't handle non-finite values.
Results may differ from a plain program's by a relative error of at most 0.0036.
Values may be sent and summed in bfloat16 or wider, within the bound.
A program may use at most 64 MiB of HBM per device.

v0:
```python
import jax
import jax.numpy as jnp
from jax import lax
from jax.sharding import PartitionSpec as P

MODEL_WIDTH = 1024


def local(
    resid,
    prenorm_gain,
    prenorm_bias,
    up_weight,
    up_bias,
    down_weight,
    down_bias,
    post_gain,
    post_bias,
    projection,
    texts,
    labels,
    step_size,
):
    feature_width = resid.shape[1]
    shift_amount = lax.axis_index("txt") * feature_width
    gathered = lax.all_gather(resid, "txt", axis=1, tiled=True)
    input_rows = gathered.astype(jnp.float32)
    input_mean = jnp.mean(input_rows, axis=1, keepdims=True)
    var_in = jnp.mean(input_rows * input_rows, axis=1, keepdims=True) - input_mean * input_mean
    input_inverse_deviation = lax.rsqrt(var_in + 1e-05)
    centered_input = (input_rows - input_mean) * input_inverse_deviation
    normed_input = (centered_input * prenorm_gain + prenorm_bias).astype(jnp.bfloat16)
    w_up = lax.all_gather(up_weight, "dp", axis=0, tiled=True)
    w_down = lax.all_gather(down_weight, "dp", axis=1, tiled=True)
    pre_act = jnp.dot(normed_input, w_up, preferred_element_type=jnp.float32) + up_bias
    gate_sig = jax.nn.sigmoid(1.702 * pre_act)
    hidden = (pre_act * gate_sig).astype(jnp.bfloat16)
    mixed_part = jnp.dot(hidden, w_down, preferred_element_type=jnp.float32)
    mixed = lax.psum_scatter(mixed_part, "txt", scatter_dimension=1, tiled=True)
    own_rows = resid.astype(jnp.float32)
    block_out = own_rows + mixed + lax.dynamic_slice_in_dim(down_bias, shift_amount, feature_width)
    out_sums = lax.psum((jnp.sum(block_out, axis=1), jnp.sum(block_out * block_out, axis=1)), "txt")
    mean_out = out_sums[0][:, None] / MODEL_WIDTH
    var_out = out_sums[1][:, None] / MODEL_WIDTH - mean_out * mean_out
    rstd_out = lax.rsqrt(var_out + 1e-05)
    yhat = (block_out - mean_out) * rstd_out
    post_normed = (yhat * post_gain + post_bias).astype(jnp.bfloat16)
    emb_part = jnp.dot(post_normed, projection, preferred_element_type=jnp.float32)
    embedding = lax.psum_scatter(emb_part, "txt", scatter_dimension=0, tiled=True)
    emb_norm = jnp.sqrt(jnp.sum(embedding * embedding, axis=1, keepdims=True) + 1e-06)
    unit_vec = embedding / emb_norm
    unit_low = lax.all_gather(unit_vec.astype(jnp.bfloat16), "txt", axis=0, tiled=True)
    text_f = texts.astype(jnp.float32)
    text_unit = (text_f / jnp.sqrt(jnp.sum(text_f * text_f, axis=1, keepdims=True) + 1e-06)).astype(
        jnp.bfloat16
    )
    logits = 100.0 * jnp.einsum(
        "ie,je->ij", unit_low, text_unit, preferred_element_type=jnp.float32
    )
    local_top = jnp.max(logits, axis=1)
    row_top = lax.pmax(local_top, "txt")
    exponent = jnp.exp(logits - row_top[:, None])
    row_total = lax.psum(jnp.sum(exponent, axis=1), "txt")
    prob = exponent / row_total[:, None]
    local_label = labels - lax.axis_index("txt") * texts.shape[0]
    columns = lax.broadcasted_iota(jnp.int32, logits.shape, 1)
    target = (columns == local_label[:, None]).astype(jnp.float32)
    score_grad = (100.0 * (prob - target)).astype(jnp.bfloat16)
    back_part = jnp.dot(score_grad, text_unit, preferred_element_type=jnp.float32)
    unit_grad = lax.psum_scatter(back_part, "txt", scatter_dimension=0, tiled=True)
    along = jnp.sum(unit_vec * unit_grad, axis=1, keepdims=True)
    grad_share = ((unit_grad - unit_vec * along) / emb_norm).astype(jnp.bfloat16)
    emb_grad = lax.all_gather(grad_share, "txt", axis=0, tiled=True)
    post_grad = jnp.einsum("ie,de->id", emb_grad, projection, preferred_element_type=jnp.float32)
    scaled = post_grad * post_gain
    back_sums = lax.psum((jnp.sum(scaled, axis=1), jnp.sum(scaled * yhat, axis=1)), "txt")
    output_gradient = (
        scaled - back_sums[0][:, None] / MODEL_WIDTH - yhat * (back_sums[1][:, None] / MODEL_WIDTH)
    ) * rstd_out
    out_full = lax.all_gather(output_gradient.astype(jnp.bfloat16), "txt", axis=1, tiled=True)
    hid_grad = jnp.einsum("id,fd->if", out_full, w_down, preferred_element_type=jnp.float32)
    act_grad = (hid_grad * (gate_sig + 1.702 * pre_act * gate_sig * (1.0 - gate_sig))).astype(
        jnp.bfloat16
    )
    normed_part = jnp.einsum("if,df->id", act_grad, w_up, preferred_element_type=jnp.float32)
    normed_gradient = lax.psum_scatter(normed_part, "txt", scatter_dimension=1, tiled=True)
    centered_input_portion = lax.dynamic_slice_in_dim(
        centered_input, shift_amount, feature_width, 1
    )
    scaled_input = normed_gradient * lax.dynamic_slice_in_dim(
        prenorm_gain, shift_amount, feature_width
    )
    input_row_sums = lax.psum(
        (jnp.sum(scaled_input, axis=1), jnp.sum(scaled_input * centered_input_portion, axis=1)),
        "txt",
    )
    input_gradient = (
        output_gradient
        + (
            scaled_input
            - input_row_sums[0][:, None] / MODEL_WIDTH
            - centered_input_portion * (input_row_sums[1][:, None] / MODEL_WIDTH)
        )
        * input_inverse_deviation
    )
    square_sum = lax.psum(jnp.sum(input_gradient * input_gradient, axis=1), "txt")
    grad_rms = jnp.sqrt(square_sum[:, None] / MODEL_WIDTH + 1e-06)
    return own_rows + step_size[0] * input_gradient / grad_rms


def solution(mesh):
    placed = (
        P("dp", "txt"),
        P(),
        P(),
        P("dp", "txt"),
        P("txt"),
        P("txt", "dp"),
        P(),
        P("txt"),
        P("txt"),
        P("txt", None),
        P("txt", None),
        P("dp"),
        P(),
    )
    return jax.shard_map(
        local, mesh=mesh, in_specs=placed, out_specs=P("dp", "txt"), check_vma=False
    )
```

profile of v0, /device:TPU:0, one launch (start us, length us, event | category | flops | bytes accessed | tf_op | source)
XLA Modules:
  0.0 297.3 jit_solution(12234471146780298693)
XLA Ops:
  6.5 0.7 all-gather.3.cloned.1.call-update
  7.3 0.0 all-gather.5.cloned.1.call-start
  7.3 0.7 all-gather.5.cloned.1.call-update
  8.0 0.0 reduce-scatter.5.cloned.1.call-start
  8.1 8.9 %all_gather.18 = bf16[256,1024]{1,0:T(8,128)(2,1)S(1)} all-gather(bf16[256,256]{1,0:T(8,128)(2,1)} %param.13), channel_id=1, replica_groups=mesh['dp'=8,'txt'=4] {'txt'}, dimensions={1}, use_global_device_ids=true | all-gather | bytes 655360 | tf_op jit(solution)/shard_map/all_gather | solution.py:26
  16.9 0.2 convert_reduce_fusion
  17.2 44.1 %all-gather.3.cloned.1.call-done = bf16[1024,1024]{1,0:T(8,128)(2,1)} async-done(((bf16[128,1024]{1,0:T(8,128)(2,1)}), bf16[1024,1024]{1,0:T(8,128)(2,1)}) %all-gather.3.cloned.1.call-update) | async-done | bytes 2097168 | tf_op jit(solution)/shard_map/all_gather | solution.py:33
  61.3 2.4 convolution_add_fusion
  63.7 48.5 %all-gather.5.cloned.1.call-done = bf16[1024,1024]{1,0:T(8,128)(2,1)} async-done(((bf16[1024,128]{1,0:T(8,128)(2,1)}), bf16[1024,1024]{1,0:T(8,128)(2,1)}) %all-gather.5.cloned.1.call-update) | async-done | bytes 2097168 | tf_op jit(solution)/shard_map/all_gather | solution.py:34
  112.3 3.3 %fusion.17 = f32[256,1024]{1,0:T(8,128)} fusion(bf16[1024,1024]{1,0:T(8,128)(2,1)} %all-gather.5.cloned.1.call-done, f32[256,1024]{1,0:T(8,128)S(1)} %convolution_add_fusion), kind=kOutput, calls=%fused_computation.32 | convolution fusion | flops 538443776 | bytes 4194304 | tf_op jit(solution)/shard_map/dot_general | solution.py:38
  115.6 0.0 reduce-scatter.5.cloned.1.call-update
  115.6 0.0 reduce-scatter.7.cloned.1.call-start
  115.7 0.9 dynamic_slice.9
  116.6 22.2 %reduce-scatter.5.cloned.1.call-done = f32[256,256]{1,0:T(8,128)} async-done(((f32[256,1024]{1,0:T(8,128)}), f32[256,256]{1,0:T(8,128)}) %reduce-scatter.5.cloned.1.call-update) | async-done | bytes 262160 | tf_op jit(solution)/shard_map/reduce_scatter | solution.py:39
  138.7 1.1 fusion.38
  139.8 5.8 %all-reduce.2 = (f32[256]{0:T(256)S(1)}, f32[256]{0:T(256)S(1)}) all-reduce(f32[256]{0:T(256)S(1)} %get-tuple-element.12, f32[256]{0:T(256)S(1)} %get-tuple-element.11), channel_id=1, replica_groups=mesh['dp'=8,'txt'=4] {'txt'}, use_global_device_ids=true, to_apply=%region_6.0 | all-reduce | flops 512 | bytes 4096 | tf_op jit(solution)/shard_map/psum | solution.py:42
  145.6 1.2 fusion.25
  146.9 0.0 reduce-scatter.7.cloned.1.call-update
  146.9 0.0 reduce-scatter.9.cloned.1.call-start
  147.0 0.5 fusion
  147.4 1.7 fusion.1
  149.2 21.7 %reduce-scatter.7.cloned.1.call-done = f32[64,768]{1,0:T(8,128)} async-done(((f32[256,768]{1,0:T(8,128)}), f32[64,768]{1,0:T(8,128)}) %reduce-scatter.7.cloned.1.call-update) | async-done | bytes 196624 | tf_op jit(solution)/shard_map/reduce_scatter | solution.py:49
  170.9 1.0 multiply_reduce_fusion.6
  171.9 1.0 fusion.35
  173.0 6.1 %all_gather.21 = bf16[256,768]{1,0:T(8,128)(2,1)S(1)} all-gather(bf16[64,768]{1,0:T(8,128)(2,1)S(1)} %fusion.35), channel_id=1, replica_groups=mesh['dp'=8,'txt'=4] {'txt'}, dimensions={0}, use_global_device_ids=true | all-gather | bytes 491520 | tf_op jit(solution)/shard_map/all_gather | solution.py:52
  179.1 3.5 %fusion.41 = (f32[256]{0:T(256)S(1)}, f32[256,1280]{1,0:T(8,128)}) fusion(bf16[256,768]{1,0:T(8,128)(2,1)S(1)} %all_gather.21, bf16[1280,768]{1,0:T(8,128)(2,1)} %fusion.1), kind=kOutput, calls=%fused_computation.81 | convolution fusion | flops 503971584 | bytes 3671040 | tf_op jit(solution)/shard_map/ie,je->ij/dot_general | solution.py:57
  182.6 6.4 %pmax.7 = f32[256]{0:T(256)S(1)} all-reduce(f32[256]{0:T(256)S(1)} %get-tuple-element.28), channel_id=1, replica_groups=mesh['dp'=8,'txt'=4] {'txt'}, use_global_device_ids=true, to_apply=%region_11.0 | all-reduce | flops 256 | bytes 2048 | tf_op jit(solution)/shard_map/pmax | solution.py:61
  189.0 1.6 fusion.3
  190.7 5.7 %psum.58 = f32[256]{0:T(256)S(1)} all-reduce(f32[256]{0:T(256)S(1)} %fusion.3), channel_id=1, replica_groups=mesh['dp'=8,'txt'=4] {'txt'}, use_global_device_ids=true, to_apply=%region_13.0 | all-reduce | flops 256 | bytes 2048 | tf_op jit(solution)/shard_map/psum | solution.py:63
  196.3 3.2 %fusion.12 = f32[256,768]{1,0:T(8,128)} fusion(bf16[1280,768]{1,0:T(8,128)(2,1)S(1)} %copy-done.2, f32[256,1280]{1,0:T(8,128)} %get-tuple-element.29, s32[256]{0:T(256)S(1)} %broadcast_subtract_fusion, f32[256]{0:T(256)S(1)} %psum.58, f32[256]{0:T(256)S(1)} %pmax.7), kind=kOutput, calls=%fused_computation.27 | convolution fusion | flops 505610240 | bytes 4066304 | tf_op jit(solution)/shard_map/dot_general | solution.py:69
  199.5 0.0 reduce-scatter.11.cloned.1.call-start
  199.6 23.9 %reduce-scatter.9.cloned.1.call-done = f32[64,768]{1,0:T(8,128)} async-done(((f32[256,768]{1,0:T(8,128)}), f32[64,768]{1,0:T(8,128)}) %reduce-scatter.9.cloned.1.call-update) | async-done | bytes 196624 | tf_op jit(solution)/shard_map/reduce_scatter | solution.py:70
  223.5 1.1 multiply_reduce_fusion.5
  224.6 1.1 divide_convert_fusion
  225.8 6.1 %all_gather.22 = bf16[256,768]{1,0:T(8,128)(2,1)S(1)} all-gather(bf16[64,768]{1,0:T(8,128)(2,1)S(1)} %divide_convert_fusion), channel_id=1, replica_groups=mesh['dp'=8,'txt'=4] {'txt'}, dimensions={0}, use_global_device_ids=true | all-gather | bytes 491520 | tf_op jit(solution)/shard_map/all_gather | solution.py:73
  231.9 0.4 fusion.37
  232.3 6.5 %all-reduce.1 = (f32[256]{0:T(256)S(1)}, f32[256]{0:T(256)S(1)}) all-reduce(f32[256]{0:T(256)S(1)} %get-tuple-element.10, f32[256]{0:T(256)S(1)} %get-tuple-element.9), channel_id=1, replica_groups=mesh['dp'=8,'txt'=4] {'txt'}, use_global_device_ids=true, to_apply=%region_19.0 | all-reduce | flops 512 | bytes 4096 | tf_op jit(solution)/shard_map/psum | solution.py:76
  238.8 0.2 fusion.39
  239.0 6.9 %all_gather.23 = bf16[256,1024]{1,0:T(8,128)(2,1)S(1)} all-gather(bf16[256,256]{1,0:T(8,128)(2,1)S(1)} %get-tuple-element.21), channel_id=1, replica_groups=mesh['dp'=8,'txt'=4] {'txt'}, dimensions={1}, use_global_device_ids=true | all-gather | bytes 655360 | tf_op jit(solution)/shard_map/all_gather | solution.py:80
  245.9 4.7 %fusion.4 = f32[256,1024]{1,0:T(8,128)} fusion(bf16[1024,1024]{1,0:T(8,128)(2,1)} %all-gather.3.cloned.1.call-done, bf16[256,1024]{1,0:T(8,128)(2,1)S(1)} %all_gather.23, bf16[1024,1024]{1,0:T(8,128)(2,1)} %all-gather.5.cloned.1.call-done, f32[256,1024]{1,0:T(8,128)S(1)} %copy-done.9), kind=kOutput, calls=%fused_computation.16 | convolution fusion | flops 1076363264 | bytes 6815744 | tf_op jit(solution)/shard_map/if,df->id/dot_general | solution.py:85
  250.6 0.8 dynamic_slice.10
  252.0 0.2 fusion.5
  252.3 23.6 %reduce-scatter.11.cloned.1.call-done = f32[256,256]{1,0:T(8,128)} async-done(((f32[256,1024]{1,0:T(8,128)}), f32[256,256]{1,0:T(8,128)}) %reduce-scatter.11.cloned.1.call-update) | async-done | bytes 262160 | tf_op jit(solution)/shard_map/reduce_scatter | solution.py:86
  275.8 1.1 multiply_reduce_fusion.4
  276.9 5.8 %all-reduce = (f32[256]{0:T(256)S(1)}, f32[256]{0:T(256)S(1)}) all-reduce(f32[256]{0:T(256)S(1)} %get-tuple-element.8, f32[256]{0:T(256)S(1)} %get-tuple-element.7), channel_id=1, replica_groups=mesh['dp'=8,'txt'=4] {'txt'}, use_global_device_ids=true, to_apply=%region_24.0 | all-reduce | flops 512 | bytes 4096 | tf_op jit(solution)/shard_map/psum | solution.py:93
  282.7 1.2 multiply_reduce_fusion
  283.9 5.7 %psum.63 = f32[256]{0:T(256)S(1)} all-reduce(f32[256]{0:T(256)S(1)} %get-tuple-element.19), channel_id=1, replica_groups=mesh['dp'=8,'txt'=4] {'txt'}, use_global_device_ids=true, to_apply=%region_26.0 | all-reduce | flops 256 | bytes 2048 | tf_op jit(solution)/shard_map/psum | solution.py:106
  289.6 0.8 convert_add_fusion
  (32 shorter events, 0.1 us)
Async XLA Ops:
  6.5 139.1 %copy-start = (bf16[256,768]{1,0:T(8,128)(2,1)S(1)}, bf16[256,768]{1,0:T(8,128)(2,1)}, u32[]{:S(2)}) copy-start(bf16[256,768]{1,0:T(8,128)(2,1)} %param.22) | copy-start | bytes 1179652
  6.5 54.8 %all-gather.3.cloned.1.call-start = ((), (), s32[]{:S(2)}) async-start(), calls=%async_computation.4 | async-start | bytes 2359296 | tf_op jit(solution)/shard_map/all_gather | solution.py:33
  7.3 105.0 %all-gather.5.cloned.1.call-start = ((), (), s32[]{:S(2)}) async-start(), calls=%async_computation.5 | async-start | bytes 2359296 | tf_op jit(solution)/shard_map/all_gather | solution.py:34
  8.0 130.7 %reduce-scatter.5.cloned.1.call-start = ((), (), s32[]{:S(2)}) async-start(), calls=%async_computation.6 | async-start | bytes 1310720 | tf_op jit(solution)/shard_map/reduce_scatter | solution.py:39
  63.7 51.9 %copy-start.8 = (f32[256,1024]{1,0:T(8,128)}, f32[256,1024]{1,0:T(8,128)S(1)}, u32[]{:S(2)}) copy-start(f32[256,1024]{1,0:T(8,128)S(1)} %convolution_add_fusion) | copy-start | bytes 3145732
  63.7 75.0 %copy-start.4 = (bf16[256,256]{1,0:T(8,128)(2,1)S(1)}, bf16[256,256]{1,0:T(8,128)(2,1)}, u32[]{:S(2)}) copy-start(bf16[256,256]{1,0:T(8,128)(2,1)} %param.13) | copy-start | bytes 393220
  63.7 81.9 %copy-start.5 = (f32[256]{0:T(256)S(1)}, f32[256]{0:T(256)}, u32[]{:S(2)}) copy-start(f32[256]{0:T(256)} %param.20) | copy-start | bytes 3076
  63.7 81.9 %copy-start.7 = (f32[256]{0:T(256)S(1)}, f32[256]{0:T(256)}, u32[]{:S(2)}) copy-start(f32[256]{0:T(256)} %param.21) | copy-start | bytes 3076
  115.6 31.4 %copy-start.6 = (s32[256]{0:T(256)S(1)}, s32[256]{0:T(256)}, u32[]{:S(2)}) copy-start(s32[256]{0:T(256)} %param.24) | copy-start | bytes 3076
  115.6 31.4 %copy-start.1 = (bf16[1280,768]{1,0:T(8,128)(2,1)S(1)}, bf16[1280,768]{1,0:T(8,128)(2,1)}, u32[]{:S(2)}) copy-start(bf16[1280,768]{1,0:T(8,128)(2,1)} %param.23) | copy-start | bytes 5898244
  115.6 55.3 %reduce-scatter.7.cloned.1.call-start = ((), (), s32[]{:S(2)}) async-start(), calls=%async_computation.7 | async-start | bytes 983040 | tf_op jit(solution)/shard_map/reduce_scatter | solution.py:49
  146.9 76.6 %reduce-scatter.9.cloned.1.call-start = ((), (), s32[]{:S(2)}) async-start(), calls=%async_computation.8 | async-start | bytes 983040 | tf_op jit(solution)/shard_map/reduce_scatter | solution.py:70
  179.1 17.2 %copy-start.2 = (bf16[1280,768]{1,0:T(8,128)(2,1)S(1)}, bf16[1280,768]{1,0:T(8,128)(2,1)}, u32[]{:S(2)}) copy-start(bf16[1280,768]{1,0:T(8,128)(2,1)} %fusion.1) | copy-start | bytes 5898244
  196.3 27.2 %copy-start.3 = (f32[64,768]{1,0:T(8,128)S(1)}, f32[64,768]{1,0:T(8,128)}, u32[]{:S(2)}) copy-start(f32[64,768]{1,0:T(8,128)} %reduce-scatter.7.cloned.1.call-done) | copy-start | bytes 589828
  199.5 76.3 %reduce-scatter.11.cloned.1.call-start = ((), (), s32[]{:S(2)}) async-start(), calls=%async_computation.9 | async-start | bytes 1310720 | tf_op jit(solution)/shard_map/reduce_scatter | solution.py:86
  224.6 21.2 %copy-start.9 = (f32[256,1024]{1,0:T(8,128)S(1)}, f32[256,1024]{1,0:T(8,128)}, u32[]{:S(2)}) copy-start(f32[256,1024]{1,0:T(8,128)} %copy-done.8) | copy-start | bytes 3145732
Sparse Core Ops, SparseCore 0:
  9.5 51.8 all-gather.2
  63.4 48.8 all-gather.4
  115.7 22.9 reduce-scatter.4
  147.0 23.8 reduce-scatter.6
  199.6 23.8 reduce-scatter.8
  250.7 25.0 reduce-scatter.10
where the time goes:
time: 298 us; the launch traced here: 297 us
  waiting for transfers between devices  185 us (62%)
  blocking collectives  63.8 us (21%)
  matrix products  18.7 us (6%)
  between operations  14.3 us (5%)
  other arithmetic  13.1 us (4%)
    all_gather x1, waiting for transfers between devices, local(): w_down = lax.all_gather(down_weight, 'dp', axis=1, tiled=True)  48.5 us
    all_gather x1, waiting for transfers between devices, local(): w_up = lax.all_gather(up_weight, 'dp', axis=0, tiled=True)  44.1 us
    reduce_scatter x1, waiting for transfers between devices, local(): lax.psum_scatter(back_part, 'txt', scatter_dimension=0, tiled=True)  23.9 us
    reduce_scatter x1, waiting for transfers between devices, local(): lax.psum_scatter(normed_part, 'txt', scatter_dimension=1, tiled=True)  23.6 us
    reduce_scatter x1, waiting for transfers between devices, local(): mixed = lax.psum_scatter(mixed_part, 'txt', scatter_dimension=1, tiled=True)  22.2 us
    reduce_scatter x1, waiting for transfers between devices, local(): lax.psum_scatter(emb_part, 'txt', scatter_dimension=0, tiled=True)  21.7 us
    all_gather x1, blocking collectives, local(): gathered = lax.all_gather(resid, 'txt', axis=1, tiled=True)  8.89 us
    all_gather x1, blocking collectives, local(): lax.all_gather(output_gradient.astype(jnp.bfloat16), 'txt', axis=1, tiled...  6.85 us
  transfers between devices with their start and end apart: 6, of which 6 were waited for; matrix products, arithmetic and copies ran while one was open for 2% of the time, Pallas kernels for 0%

commit v1 on v0

--- a/solution.py
+++ b/solution.py
@@ -31,7 +31,12 @@
     centered_input = (input_rows - input_mean) * input_inverse_deviation
     normed_input = (centered_input * prenorm_gain + prenorm_bias).astype(jnp.bfloat16)
     w_up = lax.all_gather(up_weight, "dp", axis=0, tiled=True)
-    w_down = lax.all_gather(down_weight, "dp", axis=1, tiled=True)
+    ring = [down_weight]
+    for hop in range(7):
+        ring.append(lax.ppermute(ring[-1], "dp", [(dev, (dev + 1) % 8) for dev in range(8)]))
+    w_down = jnp.roll(
+        jnp.concatenate(ring[::-1], axis=1), (lax.axis_index("dp") + 1) * ring[0].shape[1], axis=1
+    )
     pre_act = jnp.dot(normed_input, w_up, preferred_element_type=jnp.float32) + up_bias
     gate_sig = jax.nn.sigmoid(1.702 * pre_act)
     hidden = (pre_act * gate_sig).astype(jnp.bfloat16)

time: 298 us -> 295 us (0.990)
  waiting for transfers between devices: 185 us -> 169 us
  local copies, waits for them, and re-layouts: 1.7 us -> 13.9 us
    ppermute x0 -> x7, waiting for transfers between devices: none -> 77.1 us  [local(): lax.ppermute(ring[-1], 'dp', [(dev, (dev + 1) % 8) for dev in range(8)])]
    all_gather x1 -> x0, waiting for transfers between devices: 48.5 us -> none  [local(): w_down = lax.all_gather(down_weight, 'dp', axis=1, tiled=True)]
    all_gather x1, waiting for transfers between devices: 44.1 us -> 0.01 us  [local(): w_up = lax.all_gather(up_weight, 'dp', axis=0, tiled=True)]
    unnamed x20 -> x43, local copies, waits for them, and re-layouts: 0.05 us -> 12.4 us
    ppermute x0 -> x7, starting transfers between devices: none -> 2.98 us  [local(): lax.ppermute(ring[-1], 'dp', [(dev, (dev + 1) % 8) for dev in range(8)])]
  transfers between devices with their start and end apart: 6 -> 12, of which waited for: 6 -> 11; matrix products, arithmetic and copies ran while one was open for 2% -> 5% of each run, Pallas kernels for 0% -> 0%
where the time goes in v1:
time: 295 us; the launch traced here: 294 us
  waiting for transfers between devices  169 us (57%)
  blocking collectives  62.3 us (21%)
  matrix products  18.9 us (6%)
  between operations  14 us (5%)
  local copies, waits for them, and re-layouts  13.9 us (5%)
  other arithmetic  13 us (4%)
  starting transfers between devices  3.15 us (1%)
    ppermute x7, waiting for transfers between devices, local(): lax.ppermute(ring[-1], 'dp', [(dev, (dev + 1) % 8) for dev in range(8)])  77.1 us
    reduce_scatter x1, waiting for transfers between devices, local(): lax.psum_scatter(normed_part, 'txt', scatter_dimension=1, tiled=True)  24.2 us
    reduce_scatter x1, waiting for transfers between devices, local(): lax.psum_scatter(back_part, 'txt', scatter_dimension=0, tiled=True)  23.9 us
    reduce_scatter x1, waiting for transfers between devices, local(): mixed = lax.psum_scatter(mixed_part, 'txt', scatter_dimension=1, tiled=True)  21.9 us
    reduce_scatter x1, waiting for transfers between devices, local(): lax.psum_scatter(emb_part, 'txt', scatter_dimension=0, tiled=True)  21.7 us
    unnamed x43, local copies, waits for them, and re-layouts  12.4 us
    all_gather x1, blocking collectives, local(): gathered = lax.all_gather(resid, 'txt', axis=1, tiled=True)  7.42 us
    all_gather x1, blocking collectives, local(): lax.all_gather(output_gradient.astype(jnp.bfloat16), 'txt', axis=1, tiled...  6.85 us
  transfers between devices with their start and end apart: 12, of which 11 were waited for; matrix products, arithmetic and copies ran while one was open for 5% of the time, Pallas kernels for 0%

profile of v1, /device:TPU:0, one launch (start us, length us, event | category | flops | bytes accessed | tf_op | source)
XLA Modules:
  0.0 294.3 jit_solution(16642486355228864485)
XLA Ops:
  6.5 3.0 %collective-permute-start = (bf16[1024,128]{1,0:T(8,128)(2,1)}, bf16[1024,128]{1,0:T(8,128)(2,1)S(1)}, u32[]{:S(2)}, u32[]{:S(2)}) collective-permute-start(bf16[1024,128]{1,0:T(8,128)(2,1)} %param.18), channel_id=1, source_target_pairs={{0,4},{4,8},{8,12},{12,16},{16,20},{20,24},{24,28},{28,0},{1,5},{5... | collective-permute-start | bytes 786440 | tf_op jit(solution)/shard_map/ppermute | solution.py:36
  9.6 9.5 %collective-permute-done = bf16[1024,128]{1,0:T(8,128)(2,1)S(1)} collective-permute-done((bf16[1024,128]{1,0:T(8,128)(2,1)}, bf16[1024,128]{1,0:T(8,128)(2,1)S(1)}, u32[]{:S(2)}, u32[]{:S(2)}) %collective-permute-start) | collective-permute-done | bytes 262176 | tf_op jit(solution)/shard_map/ppermute | solution.py:36
  19.1 15.3 %collective-permute-done.1 = bf16[1024,128]{1,0:T(8,128)(2,1)S(1)} collective-permute-done((bf16[1024,128]{1,0:T(8,128)(2,1)S(1)}, bf16[1024,128]{1,0:T(8,128)(2,1)S(1)}, u32[]{:S(2)}, u32[]{:S(2)}) %collective-permute-start.1) | collective-permute-done | bytes 262176 | tf_op jit(solution)/shard_map/ppermute | solution.py:36
  34.4 9.1 %collective-permute-done.2 = bf16[1024,128]{1,0:T(8,128)(2,1)S(1)} collective-permute-done((bf16[1024,128]{1,0:T(8,128)(2,1)S(1)}, bf16[1024,128]{1,0:T(8,128)(2,1)S(1)}, u32[]{:S(2)}, u32[]{:S(2)}) %collective-permute-start.2) | collective-permute-done | bytes 262176 | tf_op jit(solution)/shard_map/ppermute | solution.py:36
  43.5 16.1 %collective-permute-done.3 = bf16[1024,128]{1,0:T(8,128)(2,1)S(1)} collective-permute-done((bf16[1024,128]{1,0:T(8,128)(2,1)S(1)}, bf16[1024,128]{1,0:T(8,128)(2,1)S(1)}, u32[]{:S(2)}, u32[]{:S(2)}) %collective-permute-start.3) | collective-permute-done | bytes 262176 | tf_op jit(solution)/shard_map/ppermute | solution.py:36
  59.6 15.9 %collective-permute-done.4 = bf16[1024,128]{1,0:T(8,128)(2,1)S(1)} collective-permute-done((bf16[1024,128]{1,0:T(8,128)(2,1)S(1)}, bf16[1024,128]{1,0:T(8,128)(2,1)S(1)}, u32[]{:S(2)}, u32[]{:S(2)}) %collective-permute-start.4) | collective-permute-done | bytes 262176 | tf_op jit(solution)/shard_map/ppermute | solution.py:36
  75.5 7.4 %all_gather.15 = bf16[256,1024]{1,0:T(8,128)(2,1)S(1)} all-gather(bf16[256,256]{1,0:T(8,128)(2,1)} %param.13), channel_id=1, replica_groups=mesh['dp'=8,'txt'=4] {'txt'}, dimensions={1}, use_global_device_ids=true | all-gather | bytes 655360 | tf_op jit(solution)/shard_map/all_gather | solution.py:26
  82.9 1.6 collective-permute-done.5
  84.9 9.6 %collective-permute-done.6 = bf16[1024,128]{1,0:T(8,128)(2,1)S(1)} collective-permute-done((bf16[1024,128]{1,0:T(8,128)(2,1)S(1)}, bf16[1024,128]{1,0:T(8,128)(2,1)S(1)}, u32[]{:S(2)}, u32[]{:S(2)}) %collective-permute-start.6) | collective-permute-done | bytes 262176 | tf_op jit(solution)/shard_map/ppermute | solution.py:36
  94.5 0.8 constant_dynamic-update-slice_fusion.15
  95.2 0.8 constant_dynamic-update-slice_fusion.14
  96.0 0.8 constant_dynamic-update-slice_fusion.13
  97.5 0.8 constant_dynamic-update-slice_fusion.11
  99.0 0.8 constant_dynamic-update-slice_fusion.9
  99.8 0.8 constant_dynamic-update-slice_fusion.8
  101.3 0.8 constant_dynamic-update-slice_fusion.6
  103.6 0.8 constant_dynamic-update-slice_fusion.3
  106.6 2.3 convolution_add_fusion
  108.9 1.0 copy-done.12
  109.9 3.5 %fusion.4 = f32[256,1024]{1,0:T(8,128)} fusion(bf16[1024,2048]{1,0:T(8,128)(2,1)} %constant_dynamic-update-slice_fusion, s32[]{:T(128)S(6)} %select_n.19, f32[256,1024]{1,0:T(8,128)S(1)} %convolution_add_fusion), kind=kOutput, calls=%fused_computation.7 | convolution fusion | flops 538443776 | bytes 4194308 | tf_op jit(solution)/shard_map/dot_general | solution.py:43
  113.5 0.8 dynamic_slice.14
  114.3 21.9 %reduce-scatter.5.cloned.1.call-done = f32[256,256]{1,0:T(8,128)} async-done(((f32[256,1024]{1,0:T(8,128)}), f32[256,256]{1,0:T(8,128)}) %reduce-scatter.5.cloned.1.call-update) | async-done | bytes 262160 | tf_op jit(solution)/shard_map/reduce_scatter | solution.py:44
  136.1 1.1 fusion.51
  137.2 5.8 %all-reduce.2 = (f32[256]{0:T(256)S(1)}, f32[256]{0:T(256)S(1)}) all-reduce(f32[256]{0:T(256)S(1)} %get-tuple-element.12, f32[256]{0:T(256)S(1)} %get-tuple-element.11), channel_id=1, replica_groups=mesh['dp'=8,'txt'=4] {'txt'}, use_global_device_ids=true, to_apply=%region_6.7 | all-reduce | flops 512 | bytes 4096 | tf_op jit(solution)/shard_map/psum | solution.py:47
  143.0 1.3 fusion.35
  144.9 1.7 fusion.1
  146.6 21.7 %reduce-scatter.7.cloned.1.call-done = f32[64,768]{1,0:T(8,128)} async-done(((f32[256,768]{1,0:T(8,128)}), f32[64,768]{1,0:T(8,128)}) %reduce-scatter.7.cloned.1.call-update) | async-done | bytes 196624 | tf_op jit(solution)/shard_map/reduce_scatter | solution.py:54
  168.4 1.0 multiply_reduce_fusion.6
  169.4 1.0 fusion.48
  170.4 6.1 %all_gather.17 = bf16[256,768]{1,0:T(8,128)(2,1)S(1)} all-gather(bf16[64,768]{1,0:T(8,128)(2,1)S(1)} %fusion.48), channel_id=1, replica_groups=mesh['dp'=8,'txt'=4] {'txt'}, dimensions={0}, use_global_device_ids=true | all-gather | bytes 491520 | tf_op jit(solution)/shard_map/all_gather | solution.py:57
  176.6 3.4 %fusion.54 = (f32[256]{0:T(256)S(1)}, f32[256,1280]{1,0:T(8,128)}) fusion(bf16[256,768]{1,0:T(8,128)(2,1)S(1)} %all_gather.17, bf16[1280,768]{1,0:T(8,128)(2,1)} %fusion.1), kind=kOutput, calls=%fused_computation.102 | convolution fusion | flops 503971584 | bytes 3671040 | tf_op jit(solution)/shard_map/ie,je->ij/dot_general | solution.py:62
  180.0 6.4 %pmax.7 = f32[256]{0:T(256)S(1)} all-reduce(f32[256]{0:T(256)S(1)} %get-tuple-element.28), channel_id=1, replica_groups=mesh['dp'=8,'txt'=4] {'txt'}, use_global_device_ids=true, to_apply=%region_11.12 | all-reduce | flops 256 | bytes 2048 | tf_op jit(solution)/shard_map/pmax | solution.py:66
  186.4 1.6 fusion.12
  188.1 5.7 %psum.58 = f32[256]{0:T(256)S(1)} all-reduce(f32[256]{0:T(256)S(1)} %fusion.12), channel_id=1, replica_groups=mesh['dp'=8,'txt'=4] {'txt'}, use_global_device_ids=true, to_apply=%region_13.14 | all-reduce | flops 256 | bytes 2048 | tf_op jit(solution)/shard_map/psum | solution.py:68
  193.7 3.2 %fusion.23 = f32[256,768]{1,0:T(8,128)} fusion(bf16[1280,768]{1,0:T(8,128)(2,1)S(1)} %copy-done.2, f32[256,1280]{1,0:T(8,128)} %get-tuple-element.29, s32[256]{0:T(256)S(1)} %broadcast_subtract_fusion, f32[256]{0:T(256)S(1)} %psum.58, f32[256]{0:T(256)S(1)} %pmax.7), kind=kOutput, calls=%fused_computation.31 | convolution fusion | flops 505610240 | bytes 4066304 | tf_op jit(solution)/shard_map/dot_general | solution.py:74
  197.0 23.9 %reduce-scatter.9.cloned.1.call-done = f32[64,768]{1,0:T(8,128)} async-done(((f32[256,768]{1,0:T(8,128)}), f32[64,768]{1,0:T(8,128)}) %reduce-scatter.9.cloned.1.call-update) | async-done | bytes 196624 | tf_op jit(solution)/shard_map/reduce_scatter | solution.py:75
  220.9 1.1 multiply_reduce_fusion.5
  222.0 1.0 divide_convert_fusion
  223.1 6.1 %all_gather.18 = bf16[256,768]{1,0:T(8,128)(2,1)S(1)} all-gather(bf16[64,768]{1,0:T(8,128)(2,1)S(1)} %divide_convert_fusion), channel_id=1, replica_groups=mesh['dp'=8,'txt'=4] {'txt'}, dimensions={0}, use_global_device_ids=true | all-gather | bytes 491520 | tf_op jit(solution)/shard_map/all_gather | solution.py:78
  229.7 6.5 %all-reduce.1 = (f32[256]{0:T(256)S(1)}, f32[256]{0:T(256)S(1)}) all-reduce(f32[256]{0:T(256)S(1)} %get-tuple-element.10, f32[256]{0:T(256)S(1)} %get-tuple-element.9), channel_id=1, replica_groups=mesh['dp'=8,'txt'=4] {'txt'}, use_global_device_ids=true, to_apply=%region_19.20 | all-reduce | flops 512 | bytes 4096 | tf_op jit(solution)/shard_map/psum | solution.py:81
  236.3 6.9 %all_gather.19 = bf16[256,1024]{1,0:T(8,128)(2,1)S(1)} all-gather(bf16[256,256]{1,0:T(8,128)(2,1)S(1)} %get-tuple-element.21), channel_id=1, replica_groups=mesh['dp'=8,'txt'=4] {'txt'}, dimensions={1}, use_global_device_ids=true | all-gather | bytes 655360 | tf_op jit(solution)/shard_map/all_gather | solution.py:85
  243.2 4.7 %fusion.14 = f32[256,1024]{1,0:T(8,128)} fusion(bf16[1024,1024]{1,0:T(8,128)(2,1)} %all-gather.2.cloned.1.call-done, bf16[256,1024]{1,0:T(8,128)(2,1)S(1)} %all_gather.19, bf16[1024,2048]{1,0:T(8,128)(2,1)} %constant_dynamic-update-slice_fusion, s32[]{:T(128)S(6)} %select_n.19, f32[256,1024]{1,0:T(8,128)S(1)} %copy-done.13), kind=kOutput, calls=%fused_computation.20 | convolution fusion | flops 1076363264 | bytes 6815748 | tf_op jit(solution)/shard_map/if,df->id/dot_general | solution.py:90
  248.9 24.2 %reduce-scatter.11.cloned.1.call-done = f32[256,256]{1,0:T(8,128)} async-done(((f32[256,1024]{1,0:T(8,128)}), f32[256,256]{1,0:T(8,128)}) %reduce-scatter.11.cloned.1.call-update) | async-done | bytes 262160 | tf_op jit(solution)/shard_map/reduce_scatter | solution.py:91
  273.2 1.1 multiply_reduce_fusion.4
  274.3 5.8 %all-reduce = (f32[256]{0:T(256)S(1)}, f32[256]{0:T(256)S(1)}) all-reduce(f32[256]{0:T(256)S(1)} %get-tuple-element.8, f32[256]{0:T(256)S(1)} %get-tuple-element.7), channel_id=1, replica_groups=mesh['dp'=8,'txt'=4] {'txt'}, use_global_device_ids=true, to_apply=%region_24.25 | all-reduce | flops 512 | bytes 4096 | tf_op jit(solution)/shard_map/psum | solution.py:98
  280.0 1.2 multiply_reduce_fusion
  281.3 5.7 %psum.63 = f32[256]{0:T(256)S(1)} all-reduce(f32[256]{0:T(256)S(1)} %get-tuple-element.19), channel_id=1, replica_groups=mesh['dp'=8,'txt'=4] {'txt'}, use_global_device_ids=true, to_apply=%region_26.27 | all-reduce | flops 256 | bytes 2048 | tf_op jit(solution)/shard_map/psum | solution.py:111
  286.9 0.8 convert_add_fusion
  (67 shorter events, 8.0 us)
Async XLA Ops:
  6.5 136.5 %copy-start = (bf16[256,768]{1,0:T(8,128)(2,1)S(1)}, bf16[256,768]{1,0:T(8,128)(2,1)}, u32[]{:S(2)}) copy-start(bf16[256,768]{1,0:T(8,128)(2,1)} %param.22) | copy-start | bytes 1179652
  6.5 93.2 %copy-start.5 = (bf16[1024,128]{1,0:T(8,128)(2,1)S(1)}, bf16[1024,128]{1,0:T(8,128)(2,1)}, u32[]{:S(2)}) copy-start(bf16[1024,128]{1,0:T(8,128)(2,1)} %param.18) | copy-start | bytes 786436
  6.5 100.0 %all-gather.2.cloned.1.call-start = ((), (), s32[]{:S(2)}) async-start(), calls=%async_computation.4 | async-start | bytes 2359296 | tf_op jit(solution)/shard_map/all_gather | solution.py:33
  6.5 12.5 %collective-permute-start = (bf16[1024,128]{1,0:T(8,128)(2,1)}, bf16[1024,128]{1,0:T(8,128)(2,1)S(1)}, u32[]{:S(2)}, u32[]{:S(2)}) collective-permute-start(bf16[1024,128]{1,0:T(8,128)(2,1)} %param.18), channel_id=1, source_target_pairs={{0,4},{4,8},{8,12},{12,16},{16,20},{20,24},{24,28},{28,0},{1,5},{5... | collective-permute-start | bytes 786440 | tf_op jit(solution)/shard_map/ppermute | solution.py:36
  9.5 126.6 %reduce-scatter.5.cloned.1.call-start = ((), (), s32[]{:S(2)}) async-start(), calls=%async_computation.5 | async-start | bytes 1310720 | tf_op jit(solution)/shard_map/reduce_scatter | solution.py:44
  19.1 15.3 %collective-permute-start.1 = (bf16[1024,128]{1,0:T(8,128)(2,1)S(1)}, bf16[1024,128]{1,0:T(8,128)(2,1)S(1)}, u32[]{:S(2)}, u32[]{:S(2)}) collective-permute-start(bf16[1024,128]{1,0:T(8,128)(2,1)S(1)} %collective-permute-done), channel_id=1, source_target_pairs={{0,4},{4,8},{8,12},{12,16},{16,20},{20,24},{24,28},{28,0},{1,5},{5... | collective-permute-start | bytes 786440 | tf_op jit(solution)/shard_map/ppermute | solution.py:36
  34.4 9.1 %collective-permute-start.2 = (bf16[1024,128]{1,0:T(8,128)(2,1)S(1)}, bf16[1024,128]{1,0:T(8,128)(2,1)S(1)}, u32[]{:S(2)}, u32[]{:S(2)}) collective-permute-start(bf16[1024,128]{1,0:T(8,128)(2,1)S(1)} %collective-permute-done.1), channel_id=1, source_target_pairs={{0,4},{4,8},{8,12},{12,16},{16,20},{20,24},{24,28},{28,0},{1,5},{5... | collective-permute-start | bytes 786440 | tf_op jit(solution)/shard_map/ppermute | solution.py:36
  43.5 16.1 %collective-permute-start.3 = (bf16[1024,128]{1,0:T(8,128)(2,1)S(1)}, bf16[1024,128]{1,0:T(8,128)(2,1)S(1)}, u32[]{:S(2)}, u32[]{:S(2)}) collective-permute-start(bf16[1024,128]{1,0:T(8,128)(2,1)S(1)} %collective-permute-done.2), channel_id=1, source_target_pairs={{0,4},{4,8},{8,12},{12,16},{16,20},{20,24},{24,28},{28,0},{1,5},{5... | collective-permute-start | bytes 786440 | tf_op jit(solution)/shard_map/ppermute | solution.py:36
  59.6 15.9 %collective-permute-start.4 = (bf16[1024,128]{1,0:T(8,128)(2,1)S(1)}, bf16[1024,128]{1,0:T(8,128)(2,1)S(1)}, u32[]{:S(2)}, u32[]{:S(2)}) collective-permute-start(bf16[1024,128]{1,0:T(8,128)(2,1)S(1)} %collective-permute-done.3), channel_id=1, source_target_pairs={{0,4},{4,8},{8,12},{12,16},{16,20},{20,24},{24,28},{28,0},{1,5},{5... | collective-permute-start | bytes 786440 | tf_op jit(solution)/shard_map/ppermute | solution.py:36
  75.5 9.1 %collective-permute-start.5 = (bf16[1024,128]{1,0:T(8,128)(2,1)S(1)}, bf16[1024,128]{1,0:T(8,128)(2,1)S(1)}, u32[]{:S(2)}, u32[]{:S(2)}) collective-permute-start(bf16[1024,128]{1,0:T(8,128)(2,1)S(1)} %collective-permute-done.4), channel_id=1, source_target_pairs={{0,4},{4,8},{8,12},{12,16},{16,20},{20,24},{24,28},{28,0},{1,5},{5... | collective-permute-start | bytes 786440 | tf_op jit(solution)/shard_map/ppermute | solution.py:36
  84.6 9.9 %collective-permute-start.6 = (bf16[1024,128]{1,0:T(8,128)(2,1)S(1)}, bf16[1024,128]{1,0:T(8,128)(2,1)S(1)}, u32[]{:S(2)}, u32[]{:S(2)}) collective-permute-start(bf16[1024,128]{1,0:T(8,128)(2,1)S(1)} %collective-permute-done.5), channel_id=1, source_target_pairs={{0,4},{4,8},{8,12},{12,16},{16,20},{20,24},{24,28},{28,0},{1,5},{5... | collective-permute-start | bytes 786440 | tf_op jit(solution)/shard_map/ppermute | solution.py:36
  84.8 21.7 %copy-start.9 = (f32[1024]{0:T(1024)S(1)}, f32[1024]{0:T(1024)}, u32[]{:S(2)}) copy-start(f32[1024]{0:T(1024)} %param.14) | copy-start | bytes 12292
  84.9 21.7 %copy-start.10 = (f32[1024]{0:T(1024)S(1)}, f32[1024]{0:T(1024)}, u32[]{:S(2)}) copy-start(f32[1024]{0:T(1024)} %param.17) | copy-start | bytes 12292
  84.9 21.7 %copy-start.11 = (f32[1024]{0:T(1024)S(1)}, f32[1024]{0:T(1024)}, u32[]{:S(2)}) copy-start(f32[1024]{0:T(1024)} %param.15) | copy-start | bytes 12292
  108.9 1.0 copy-start.12
  109.9 26.3 %copy-start.4 = (bf16[256,256]{1,0:T(8,128)(2,1)S(1)}, bf16[256,256]{1,0:T(8,128)(2,1)}, u32[]{:S(2)}) copy-start(bf16[256,256]{1,0:T(8,128)(2,1)} %param.13) | copy-start | bytes 393220
  109.9 33.1 %copy-start.6 = (f32[256]{0:T(256)S(1)}, f32[256]{0:T(256)}, u32[]{:S(2)}) copy-start(f32[256]{0:T(256)} %param.20) | copy-start | bytes 3076
  109.9 33.1 %copy-start.8 = (f32[256]{0:T(256)S(1)}, f32[256]{0:T(256)}, u32[]{:S(2)}) copy-start(f32[256]{0:T(256)} %param.21) | copy-start | bytes 3076
  109.9 34.5 %copy-start.7 = (s32[256]{0:T(256)S(1)}, s32[256]{0:T(256)}, u32[]{:S(2)}) copy-start(s32[256]{0:T(256)} %param.24) | copy-start | bytes 3076
  109.9 34.5 %copy-start.1 = (bf16[1280,768]{1,0:T(8,128)(2,1)S(1)}, bf16[1280,768]{1,0:T(8,128)(2,1)}, u32[]{:S(2)}) copy-start(bf16[1280,768]{1,0:T(8,128)(2,1)} %param.23) | copy-start | bytes 5898244
  113.5 54.9 %reduce-scatter.7.cloned.1.call-start = ((), (), s32[]{:S(2)}) async-start(), calls=%async_computation.6 | async-start | bytes 983040 | tf_op jit(solution)/shard_map/reduce_scatter | solution.py:54
  144.4 76.6 %reduce-scatter.9.cloned.1.call-start = ((), (), s32[]{:S(2)}) async-start(), calls=%async_computation.7 | async-start | bytes 983040 | tf_op jit(solution)/shard_map/reduce_scatter | solution.py:75
  146.6 47.1 %copy-start.2 = (bf16[1280,768]{1,0:T(8,128)(2,1)S(1)}, bf16[1280,768]{1,0:T(8,128)(2,1)}, u32[]{:S(2)}) copy-start(bf16[1280,768]{1,0:T(8,128)(2,1)} %fusion.1) | copy-start | bytes 5898244
  193.7 27.2 %copy-start.3 = (f32[64,768]{1,0:T(8,128)S(1)}, f32[64,768]{1,0:T(8,128)}, u32[]{:S(2)}) copy-start(f32[64,768]{1,0:T(8,128)} %reduce-scatter.7.cloned.1.call-done) | copy-start | bytes 589828
  196.9 46.3 %copy-start.13 = (f32[256,1024]{1,0:T(8,128)S(1)}, f32[256,1024]{1,0:T(8,128)}, u32[]{:S(2)}) copy-start(f32[256,1024]{1,0:T(8,128)} %copy-done.12) | copy-start | bytes 3145732
  196.9 76.2 %reduce-scatter.11.cloned.1.call-start = ((), (), s32[]{:S(2)}) async-start(), calls=%async_computation.8 | async-start | bytes 1310720 | tf_op jit(solution)/shard_map/reduce_scatter | solution.py:91
Sparse Core Ops, SparseCore 0:
  9.7 61.9 all-gather.1
  113.6 22.5 reduce-scatter.4
  144.5 23.8 reduce-scatter.6
  197.0 23.8 reduce-scatter.8
  248.1 25.0 reduce-scatter.10
